TPU v7x, 32 devices: a whole 2x2x4 slice. The times are simulated.
32 devices in a mesh: dp: 8 (over y, x, core), tp: 4 (over z).
Axes of the slice: x: 2, y: 2, z: 4, core: 2. Of those that a mesh axis runs over, the one named last changes fastest.
Arguments:
- resid: bfloat16 [2048, 4096], P('dp'), may hold values from -6 to 6
- gain: bfloat16 [4096], replicated, may hold values from 0.25 to 1.75
- grad_q: bfloat16 [2048, 3072], P('dp', 'tp'), may hold values from -1.25 to 1.25
- w_query: bfloat16 [3072, 4096], P('tp'), may hold values from -0.375 to 0.375
- grad_in: bfloat16 [2048, 4096], P('dp'), may hold values from -2 to 2
Outputs:
- weight_grad: float32 [3072, 4096], P(('tp', 'dp'))
- gain_grad: float32 [4096], replicated
- grad_out: bfloat16 [2048, 4096], P('dp')
All inputs are finite; a program needn't handle non-finite values.
Results may differ from a plain program's by a relative error of at most 0.014.
Values may be sent and summed in bfloat16 or wider, within the bound.
A program may use at most 128 MiB of HBM per device.

v0:
```python
import jax
import jax.numpy as jnp
from jax import lax
from jax.sharding import PartitionSpec as P


def norm_rows(rows_bf, gain_f):
    rows_f = rows_bf.astype(jnp.float32)
    inv_rms = lax.rsqrt(jnp.mean(rows_f * rows_f, axis=-1, keepdims=True) + 1e-05)
    unit = rows_f * inv_rms
    return (inv_rms, unit, (unit * gain_f).astype(jnp.bfloat16))


def per_device(resid, gain, grad_q, w_query, grad_in):
    gain_f = gain.astype(jnp.float32)
    inv_rms, unit, normed = norm_rows(resid, gain_f)
    local_term = jnp.dot(grad_q, w_query, preferred_element_type=jnp.float32)
    dnormed = lax.psum(local_term.astype(jnp.bfloat16), "tp").astype(jnp.float32)
    full_grad = lax.dot_general(
        grad_q, normed, (((0,), (0,)), ((), ())), preferred_element_type=jnp.float32
    )
    weight_grad = lax.psum_scatter(full_grad, "dp", scatter_dimension=0, tiled=True)
    gain_grad = lax.psum(jnp.sum(dnormed * unit, axis=0), "dp")
    dunit = dnormed * gain_f
    inner = jnp.mean(dunit * unit, axis=-1, keepdims=True)
    grad_rows = (grad_in.astype(jnp.float32) + inv_rms * (dunit - unit * inner)).astype(
        jnp.bfloat16
    )
    return (weight_grad, gain_grad, grad_rows)


def solution(mesh):
    return jax.shard_map(
        per_device,
        mesh=mesh,
        in_specs=(P("dp", None), P(), P("dp", "tp"), P("tp", None), P("dp", None)),
        out_specs=(P(("tp", "dp"), None), P(), P("dp", None)),
        check_vma=False,
    )
```

profile of v0, /device:TPU:0, one launch (start us, length us, event | category | flops | bytes accessed | tf_op | source)
XLA Modules:
  0.0 145.5 jit_solution(15786352697211024213)
XLA Ops:
  8.0 0.0 copy-start
  8.0 0.0 copy-start.2
  8.0 0.0 copy-start.1
  8.0 0.0 all-reduce.2.cloned.1.call-start
  8.1 0.9 copy-done
  9.0 5.9 %convolution_convert_fusion = bf16[256,4096]{1,0:T(8,128)(2,1)} fusion(bf16[256,768]{1,0:T(8,128)(2,1)S(1)} %copy-done, bf16[768,4096]{1,0:T(8,128)(2,1)} %param.8), kind=kOutput, calls=%fused_computation.8 | convolution fusion | flops 1611661312 | bytes 8781824 | tf_op jit(solution)/shard_map/dot_general | solution.py:17
  14.9 0.0 all-reduce.2.cloned.1.call-update
  14.9 0.0 reduce-scatter.4.cloned.1.call-start
  15.0 0.0 copy-done.2
  15.0 0.0 copy-done.1
  15.0 0.5 fusion.9
  15.5 6.6 %convolution_bitcast_fusion = f32[768,4096]{0,1:T(8,128)} fusion(bf16[256,768]{1,0:T(8,128)(2,1)S(1)} %copy-done, bf16[256,4096]{1,0:T(8,128)(2,1)S(1)} %copy-done.1, f32[4096]{0:T(1024)S(1)} %convert_element_type.22, f32[256]{0:T(256)S(1)} %add_rsqrt_fusion), kind=kOutput, calls=%fused_computation | convolution fusion | flops 1614807040 | bytes 15090688 | tf_op jit(solution)/shard_map/dot_general | solution.py:19
  22.1 12.9 %copy.10 = f32[768,4096]{1,0:T(8,128)} copy(f32[768,4096]{0,1:T(8,128)} %convolution_bitcast_fusion) | data formatting | bytes 25165824
  35.0 0.0 reduce-scatter.4.cloned.1.call-update
  35.1 68.9 %all-reduce.2.cloned.1.call-done = bf16[256,4096]{1,0:T(8,128)(2,1)} async-done(((bf16[256,4096]{1,0:T(8,128)(2,1)}), bf16[256,4096]{1,0:T(8,128)(2,1)}) %all-reduce.2.cloned.1.call-update) | async-done | bytes 2097168 | tf_op jit(solution)/shard_map/psum | solution.py:18
  103.9 3.3 %fusion.8 = (f32[256]{0:T(256)S(1)}, f32[4096]{0:T(1024)S(1)}) fusion(bf16[256,4096]{1,0:T(8,128)(2,1)S(1)} %copy-done.1, bf16[256,4096]{1,0:T(8,128)(2,1)} %all-reduce.2.cloned.1.call-done, f32[4096]{0:T(1024)S(1)} %convert_element_type.22, f32[256]{0:T(256)S(1)} %add_rsqrt_fusion), kind=kLoop, calls=%fused_computation.14 | loop fusion | flops 8384256 | bytes 4229120 | tf_op jit(solution)/shard_map/reduce_sum | solution.py:25
  107.2 25.7 %psum.15 = f32[4096]{0:T(1024)} all-reduce(f32[4096]{0:T(1024)S(1)} %get-tuple-element.10), channel_id=1, replica_groups=mesh['dp'=8,'tp'=4] {'dp'}, use_global_device_ids=true, to_apply=%region_4.0 | all-reduce | flops 4096 | bytes 32768 | tf_op jit(solution)/shard_map/psum | solution.py:23
  132.9 5.1 %fusion.6 = bf16[256,4096]{1,0:T(8,128)(2,1)} fusion(bf16[256,4096]{1,0:T(8,128)(2,1)} %all-reduce.2.cloned.1.call-done, bf16[256,4096]{1,0:T(8,128)(2,1)S(1)} %copy-done.1, bf16[256,4096]{1,0:T(8,128)(2,1)} %param.9, f32[256]{0:T(256)S(1)} %broadcast_multiply_fusion, f32[4096]{0:T(1024)S(1)} %convert_element_type.22, f32[256]{0:T(256)S(1)} %add_rsqrt_fusion), kind=kLoop, calls=%fused_computation.12 | loop fusion | flops 10485760 | bytes 8407040 | tf_op jit(solution)/shard_map/convert_element_type | solution.py:26
  138.0 0.0 reduce-scatter.4.cloned.1.call-done
  (3 shorter events, 0.0 us)
Async XLA Ops:
  8.0 1.0 copy-start
  8.0 7.0 %copy-start.2 = (bf16[4096]{0:T(1024)(128)(2,1)S(1)}, bf16[4096]{0:T(1024)(128)(2,1)}, u32[]{:S(2)}) copy-start(bf16[4096]{0:T(1024)(128)(2,1)} %param.6) | copy-start | bytes 24580
  8.0 7.0 %copy-start.1 = (bf16[256,4096]{1,0:T(8,128)(2,1)S(1)}, bf16[256,4096]{1,0:T(8,128)(2,1)}, u32[]{:S(2)}) copy-start(bf16[256,4096]{1,0:T(8,128)(2,1)} %param.5) | copy-start | bytes 6291460
  8.0 95.9 %all-reduce.2.cloned.1.call-start = ((), (), s32[]{:S(2)}) async-start(), calls=%async_computation.1 | async-start | bytes 4194304 | tf_op jit(solution)/shard_map/psum | solution.py:18
  14.9 123.1 %reduce-scatter.4.cloned.1.call-start = ((), (), s32[]{:S(2)}) async-start(), calls=%async_computation.2 | async-start | bytes 14155776
Sparse Core Ops, SparseCore 0:
  15.0 88.8 all-reduce.1
Sparse Core Ops, SparseCore 1:
  35.1 95.2 reduce-scatter.3
where the time goes:
time: 146 us; the launch traced here: 145 us
  waiting for transfers between devices  68.9 us (47%)
  blocking collectives  25.7 us (18%)
  between operations  15.5 us (11%)
  local copies, waits for them, and re-layouts  13.9 us (10%)
  matrix products  12.5 us (9%)
  other arithmetic  8.89 us (6%)
    psum x1, waiting for transfers between devices, per_device(): lax.psum(local_term.astype(jnp.bfloat16), 'tp').astype(jnp.float32)  68.9 us
    psum x1, blocking collectives, per_device(): gain_grad = lax.psum(jnp.sum(dnormed * unit, axis=0), 'dp')  25.7 us
    unnamed x7, local copies, waits for them, and re-layouts  13.9 us
    dot_general x1, matrix products, per_device(): lax.dot_general(grad_q, normed, (((0,), (0,)), ((), ())), preferred_eleme...  6.6 us
    dot_general x1, matrix products, per_device(): local_term = jnp.dot(grad_q, w_query, preferred_element_type=jnp.float32)  5.9 us
    convert_element_type x1, other arithmetic, per_device(): (grad_in.astype(jnp.float32) + inv_rms * (dunit - unit * inner)).astype(j...  5.12 us
    reduce_sum x1, other arithmetic, per_device(): inner = jnp.mean(dunit * unit, axis=-1, keepdims=True)  3.26 us
  transfers between devices with their start and end apart: 2, of which 1 were waited for; matrix products, arithmetic and copies ran while one was open for 20% of the time, Pallas kernels for 0%

commit v1 on v0

--- a/solution.py
+++ b/solution.py
@@ -1,7 +1,17 @@
+import functools
+
 import jax
 import jax.numpy as jnp
 from jax import lax
+from jax.experimental import pallas as pl
+from jax.experimental.pallas import tpu as pltpu
 from jax.sharding import PartitionSpec as P
+
+MESH = pl.DeviceIdType.MESH
+F32 = jnp.float32
+BF16 = jnp.bfloat16
+ROWS = 16
+TILES = 8
 
 
 def norm_rows(rows_bf, gain_f):
@@ -29,9 +39,323 @@
     return (weight_grad, gain_grad, grad_rows)
 
 
+def kernel(n_dp, n_tp, resid, gain, grad_q, w_query, grad_in, wg_out, gg_out, go_out,
+           wv, rv, gqv, giv, nv, part, from_mate, from_peer, gq_t, gq_p,
+           fgs, fgr, keep, xs, xr, ys, yr, wgo, gacc, gslot, gz,
+           w_sem, in_sem, so, ro, sp, rp, out_sem, s1, r1, s2, r2, s3, r3, wg_sem, sg, rg, sz, rz):
+    dp, tp = lax.axis_index("dp"), lax.axis_index("tp")
+    tokens, width = rv.shape
+    heads = gqv.shape[1]
+    chunks = tokens // ROWS
+    steps = chunks // 2
+    cols = width // TILES
+    block = heads // n_dp
+    h = tp // 2
+    is_inner = jnp.logical_and(tp > 0, tp < n_tp - 1)
+    is_outer = jnp.logical_not(is_inner)
+    mate = jnp.where(is_inner, h * (n_tp - 1), 1 + h)
+    peer = 2 - h
+    core, xx, yy = dp % 2, (dp // 2) % 2, dp // 4
+    core_mate = dp + 1 - 2 * core
+    x_mate = dp + 2 - 4 * xx
+    y_mate = dp + 4 - 8 * yy
+
+    def w_copy(t):
+        c = pl.ds(t * cols, cols)
+        return pltpu.make_async_copy(w_query.at[:, c], wv.at[:, c], w_sem.at[t])
+
+    gq_copy = pltpu.make_async_copy(grad_q, gqv, in_sem.at[0])
+    r_copy = pltpu.make_async_copy(resid, rv, in_sem.at[1])
+    gi_copy = pltpu.make_async_copy(grad_in, giv, in_sem.at[2])
+    gq_copy.start()
+    for t in range(TILES):
+        w_copy(t).start()
+    r_copy.start()
+    gi_copy.start()
+
+    barrier = pltpu.get_barrier_semaphore()
+    for o in range(1, n_dp):
+        pl.semaphore_signal(barrier, inc=1, device_id={"dp": (dp + o) % n_dp}, device_id_type=MESH)
+    for o in range(1, n_tp):
+        pl.semaphore_signal(barrier, inc=1, device_id={"tp": (tp + o) % n_tp}, device_id_type=MESH)
+
+    def rows_of(c):
+        return pl.ds(pl.multiple_of(c * ROWS, ROWS), ROWS)
+
+    def copy_o(src, c):
+        return pltpu.make_async_remote_copy(
+            src_ref=src.at[rows_of(c)], dst_ref=from_mate.at[rows_of(c)],
+            send_sem=so.at[c], recv_sem=ro.at[c], device_id={"tp": mate}, device_id_type=MESH)
+
+    def copy_p(src, c):
+        return pltpu.make_async_remote_copy(
+            src_ref=src.at[rows_of(c)], dst_ref=from_peer.at[rows_of(c)],
+            send_sem=sp.at[c], recv_sem=rp.at[c], device_id={"tp": peer}, device_id_type=MESH)
+
+    def out_copy(src, c):
+        return pltpu.make_async_copy(src.at[rows_of(c)], go_out.at[rows_of(c)], out_sem.at[c])
+
+    def hop(src, dst, send, recv, t, to):
+        return pltpu.make_async_remote_copy(
+            src_ref=src.at[t], dst_ref=dst.at[t], send_sem=send.at[t], recv_sem=recv.at[t],
+            device_id={"dp": to}, device_id_type=MESH)
+
+    gq_copy.wait()
+    half = tokens // 2
+    for m in range(2):
+        for t in range(TILES):
+            if m == 0:
+                w_copy(t).wait()
+            c = slice(t * cols, (t + 1) * cols)
+            r = slice(m * half, (m + 1) * half)
+            part[r, c] = jnp.dot(gqv[r, :], wv[:, c], preferred_element_type=F32).astype(BF16)
+        if m == 0:
+            pl.semaphore_wait(barrier, n_dp - 1 + n_tp - 1)
+
+        @pl.when(is_outer)
+        def _():
+            @pl.loop(m * steps // 2, (m + 1) * steps // 2)
+            def _(k):
+                copy_o(part, 2 * k + 1 - h).start()
+                copy_o(part, 2 * k + h).start()
+
+    gain_f = gain[...].astype(F32)
+    r_copy.wait()
+
+    @pl.loop(0, chunks)
+    def _(c):
+        r = rows_of(c)
+        nv[r, :] = norm_rows(rv[r, :], gain_f)[2]
+
+    gq_t[...] = gqv[...].T
+    for v in range(2):
+        for j, rel in enumerate(((0, 2, 1, 3), (0, 1, 2, 3))[v]):
+            y_to = yy + (rel // 2) * (1 - 2 * yy)
+            x_to = xx + (rel % 2) * (1 - 2 * xx)
+            for mine in range(2):
+                c_to = core if mine else 1 - core
+                at = pl.multiple_of((y_to * 4 + x_to * 2 + c_to) * block, block)
+                gq_p[v, mine, j * block:(j + 1) * block, :] = gq_t[pl.ds(at, block), :]
+    gacc[...] = jnp.zeros_like(gacc)
+    first, second = (x_mate, y_mate), (y_mate, x_mate)
+
+    def tile_cols(t):
+        return pl.ds(pl.multiple_of(t * cols, cols), cols)
+
+    @pl.loop(0, TILES // 2)
+    def _(j):
+        for v in range(2):
+            t = 2 * j + v
+            fgs[t] = jnp.dot(gq_p[v, 0], nv[:, tile_cols(t)], preferred_element_type=F32).astype(BF16)
+            hop(fgs, fgr, s1, r1, t, core_mate).start()
+
+    def stage2(j):
+        for v in range(2):
+            t = 2 * j + v
+            hop(fgs, fgr, s1, r1, t, core_mate).wait_recv()
+            total = jnp.dot(gq_p[v, 1], nv[:, tile_cols(t)], preferred_element_type=F32)
+            total = total + fgr[t].astype(F32)
+            xs[t] = total[2 * block:].astype(BF16)
+            hop(xs, xr, s2, r2, t, first[v]).start()
+            keep[t] = total[:2 * block]
+
+    def stage3(j):
+        for v in range(2):
+            t = 2 * j + v
+            hop(xs, xr, s2, r2, t, first[v]).wait_recv()
+            ys[t] = (keep[t, block:] + xr[t, block:].astype(F32)).astype(BF16)
+            hop(ys, yr, s3, r3, t, second[v]).start()
+            keep[t, :block] = keep[t, :block] + xr[t, :block].astype(F32)
+
+    def wg_copy(t):
+        return pltpu.make_async_copy(wgo.at[t], wg_out.at[:, tile_cols(t)], wg_sem.at[t])
+
+    def stage4(j):
+        for v in range(2):
+            t = 2 * j + v
+            hop(ys, yr, s3, r3, t, second[v]).wait_recv()
+            wgo[t] = keep[t, :block] + yr[t].astype(F32)
+            wg_copy(t).start()
+
+    gi_copy.wait()
+
+    def forward(k):
+        b = 2 * k + 1 - h
+        copy_p(from_peer, b).wait_recv()
+        copy_o(from_peer, b).start()
+        out_copy(from_peer, b).start()
+
+    def collect(k):
+        for c in (2 * k + h, 2 * k + 1 - h):
+            copy_o(from_mate, c).wait_recv()
+            out_copy(from_mate, c).start()
+
+    @pl.loop(0, steps)
+    def _(k):
+        @pl.when(is_inner)
+        def _():
+            a, b = 2 * k + h, 2 * k + 1 - h
+            copy_o(part, b).wait_recv()
+            part[rows_of(b), :] = (
+                part[rows_of(b), :].astype(F32) + from_mate[rows_of(b), :].astype(F32)
+            ).astype(BF16)
+            copy_p(part, b).start()
+            copy_o(part, a).wait_recv()
+            copy_p(part, a).wait_recv()
+            r = rows_of(a)
+            inv_rms, unit, _ = norm_rows(rv[r, :], gain_f)
+            dnormed = part[r, :].astype(F32) + from_mate[r, :].astype(F32)
+            dnormed = dnormed + from_peer[r, :].astype(F32)
+            gacc[...] += jnp.sum(dnormed * unit, axis=0, keepdims=True)
+            dunit = dnormed * gain_f
+            mean = jnp.mean(dunit * unit, axis=-1, keepdims=True)
+            part[r, :] = (
+                giv[r, :].astype(F32) + inv_rms * (dunit - unit * mean)
+            ).astype(BF16)
+            copy_p(part, a).start()
+            copy_o(part, a).start()
+            out_copy(part, a).start()
+
+            @pl.when(k > 0)
+            def _():
+                forward(k - 1)
+
+        @pl.when(jnp.logical_and(is_outer, k > 2))
+        def _():
+            collect(k - 3)
+
+        @pl.when(k < 2)
+        def _():
+            stage2(2 * k)
+            stage2(2 * k + 1)
+
+        @pl.when(jnp.logical_and(k >= 2, k < 2 + TILES // 2))
+        def _():
+            stage3(k - 2)
+
+        @pl.when(jnp.logical_and(k >= 4, k < 4 + TILES // 2))
+        def _():
+            stage4(k - 4)
+
+    def g_copy(o):
+        return pltpu.make_async_remote_copy(
+            src_ref=gslot.at[0], dst_ref=gslot.at[o], send_sem=sg.at[o], recv_sem=rg.at[o],
+            device_id={"dp": (dp + o) % n_dp}, device_id_type=MESH)
+
+    def z_copy(i, to):
+        return pltpu.make_async_remote_copy(
+            src_ref=gz.at[h], dst_ref=gz.at[h], send_sem=sz.at[i], recv_sem=rz.at[h],
+            device_id={"tp": to}, device_id_type=MESH)
+
+    def z_wait(which):
+        pltpu.make_async_remote_copy(
+            src_ref=gz.at[which], dst_ref=gz.at[which], send_sem=sz.at[0], recv_sem=rz.at[which],
+            device_id={"tp": mate}, device_id_type=MESH).wait_recv()
+
+    @pl.when(is_inner)
+    def _():
+        gslot[0] = gacc[...]
+        for o in range(1, n_dp):
+            g_copy(o).start()
+        forward(steps - 1)
+        for o in range(1, n_dp):
+            g_copy(o).wait_recv()
+        total = gslot[dp % n_dp]
+        for d in range(1, n_dp):
+            total = total + gslot[(dp + n_dp - d) % n_dp]
+        gz[h] = total
+        targets = (mate, peer, (1 - h) * (n_tp - 1))
+        for i, to in enumerate(targets):
+            z_copy(i, to).start()
+        z_wait(1 - h)
+        gg_out[...] = gz[0] + gz[1]
+        for i, to in enumerate(targets):
+            z_copy(i, to).wait_send()
+        for o in range(1, n_dp):
+            g_copy(o).wait_send()
+
+        @pl.loop(0, chunks)
+        def _(c):
+            copy_p(part, c).wait_send()
+
+    @pl.when(is_outer)
+    def _():
+        for k in range(steps - 3, steps):
+            collect(k)
+        z_wait(0)
+        z_wait(1)
+        gg_out[...] = gz[0] + gz[1]
+
+    @pl.loop(0, chunks)
+    def _(c):
+        copy_o(part, c).wait_send()
+        out_copy(part, c).wait()
+
+    for t in range(TILES):
+        hop(fgs, fgr, s1, r1, t, core_mate).wait_send()
+        hop(xs, xr, s2, r2, t, first[t % 2]).wait_send()
+        hop(ys, yr, s3, r3, t, second[t % 2]).wait_send()
+        wg_copy(t).wait()
+
+
+def fused(n_dp, n_tp, resid, gain, grad_q, w_query, grad_in):
+    tokens, width = resid.shape
+    heads = grad_q.shape[1]
+    chunks = tokens // ROWS
+    block, cols = heads // n_dp, width // TILES
+    any_space = pl.BlockSpec(memory_space=pl.ANY)
+    vmem = pl.BlockSpec(memory_space=pltpu.VMEM)
+    dma = lambda n: pltpu.SemaphoreType.DMA((n,))
+    weight_grad, gain_grad, grad_rows = pl.pallas_call(
+        functools.partial(kernel, n_dp, n_tp),
+        out_shape=(
+            jax.ShapeDtypeStruct((block, width), F32),
+            jax.ShapeDtypeStruct((1, width), F32),
+            jax.ShapeDtypeStruct((tokens, width), BF16),
+        ),
+        in_specs=[any_space, vmem, any_space, any_space, any_space],
+        out_specs=(any_space, vmem, any_space),
+        scratch_shapes=[
+            pltpu.VMEM((heads, width), BF16),
+            pltpu.VMEM((tokens, width), BF16),
+            pltpu.VMEM((tokens, heads), BF16),
+            pltpu.VMEM((tokens, width), BF16),
+            pltpu.VMEM((tokens, width), BF16),
+            pltpu.VMEM((tokens, width), BF16),
+            pltpu.VMEM((tokens, width), BF16),
+            pltpu.VMEM((tokens, width), BF16),
+            pltpu.VMEM((heads, tokens), BF16),
+            pltpu.VMEM((2, 2, 4 * block, tokens), BF16),
+            pltpu.VMEM((TILES, 4 * block, cols), BF16),
+            pltpu.VMEM((TILES, 4 * block, cols), BF16),
+            pltpu.VMEM((TILES, 2 * block, cols), F32),
+            pltpu.VMEM((TILES, 2 * block, cols), BF16),
+            pltpu.VMEM((TILES, 2 * block, cols), BF16),
+            pltpu.VMEM((TILES, block, cols), BF16),
+            pltpu.VMEM((TILES, block, cols), BF16),
+            pltpu.VMEM((TILES, block, cols), F32),
+            pltpu.VMEM((1, width), F32),
+            pltpu.VMEM((n_dp, 1, width), F32),
+            pltpu.VMEM((2, 1, width), F32),
+            dma(TILES), dma(3), dma(chunks), dma(chunks), dma(chunks), dma(chunks), dma(chunks),
+            dma(TILES), dma(TILES), dma(TILES), dma(TILES), dma(TILES), dma(TILES), dma(TILES),
+            dma(n_dp), dma(n_dp), dma(3), dma(2),
+        ],
+        compiler_params=pltpu.CompilerParams(
+            collective_id=0, has_side_effects=True, vmem_limit_bytes=60 * 1024 * 1024
+        ),
+    )(resid, gain.reshape(1, width), grad_q, w_query, grad_in)
+    return weight_grad, gain_grad.reshape(width), grad_rows
+
+
 def solution(mesh):
+    n_dp, n_tp = mesh.shape["dp"], mesh.shape["tp"]
+    if (n_dp, n_tp) == (2 * 2 * 2, 4):
+        body = functools.partial(fused, n_dp, n_tp)
+    else:
+        body = per_device
     return jax.shard_map(
-        per_device,
+        body,
         mesh=mesh,
         in_specs=(P("dp", None), P(), P("dp", "tp"), P("tp", None), P("dp", None)),
         out_specs=(P(("tp", "dp"), None), P(), P("dp", None)),

time: 146 us -> 83.9 us (0.57)
  Pallas kernels: 0 us -> 76.9 us
  waiting for transfers between devices: 68.9 us -> 0 us
  blocking collectives: 25.7 us -> 0 us
  between operations: 15.5 us -> 0.66 us
  matrix products: 12.5 us -> 0 us
  other arithmetic: 8.89 us -> 0 us
  local copies, waits for them, and re-layouts: 13.9 us -> 6.05 us
    pallas_call x0 -> x1, Pallas kernels: none -> 76.9 us  [fused(): pl.pallas_call(functools.partial(kernel, n_dp, n_tp), out_shape=(jax.Shap...]
    psum x1 -> x0, waiting for transfers between devices: 68.9 us -> none  [per_device(): lax.psum(local_term.astype(jnp.bfloat16), 'tp').astype(jnp.float32)]
    psum x1 -> x0, blocking collectives: 25.7 us -> none  [per_device(): gain_grad = lax.psum(jnp.sum(dnormed * unit, axis=0), 'dp')]
    dot_general x2 -> x0, matrix products: 12.5 us -> none  [the longest x1 6.6 us: per_device(): lax.dot_general(grad_q, normed, (((0,), (0,)), ((), ())), preferred_eleme...]
    unnamed x7, local copies, waits for them, and re-layouts: 13.9 us -> 4.74 us
    convert_element_type x2 -> x0, other arithmetic: 5.13 us -> none  [the longest x1 5.12 us: per_device(): (grad_in.astype(jnp.float32) + inv_rms * (dunit - unit * inner)).astype(j...]
    reduce_sum x2 -> x0, other arithmetic: 3.75 us -> none  [the longest x1 3.26 us: per_device(): inner = jnp.mean(dunit * unit, axis=-1, keepdims=True)]
  transfers between devices with their start and end apart: 2 -> 0, of which waited for: 1 -> 0; matrix products, arithmetic and copies ran while one was open for 20% -> 0% of each run, Pallas kernels for 0% -> 0%
where the time goes in v1:
time: 83.9 us; the launch traced here: 83.6 us
  Pallas kernels  76.9 us (92%)
  local copies, waits for them, and re-layouts  6.05 us (7%)
    pallas_call x1, Pallas kernels, fused(): pl.pallas_call(functools.partial(kernel, n_dp, n_tp), out_shape=(jax.Shap...  76.9 us
    unnamed x7, local copies, waits for them, and re-layouts  4.74 us

profile of v1, /device:TPU:0, one launch (start us, length us, event | category | flops | bytes accessed | tf_op | source)
XLA Modules:
  0.0 83.6 jit_solution(12709159848879381152)
XLA Ops:
  0.6 1.3 %reshape.12.gain = bf16[1,4096]{1,0:T(2,128)(2,1)} reshape(bf16[4096]{0:T(1024)(128)(2,1)} %param.6) | data formatting | bytes 16384 | tf_op jit(solution)/shard_map/reshape | solution.py:347
  1.9 76.9 %shard_map.76 = (f32[96,4096]{1,0:T(8,128)}, f32[1,4096]{1,0:T(1,128)}, bf16[256,4096]{1,0:T(8,128)(2,1)}) custom-call(bf16[256,4096]{1,0:T(8,128)(2,1)} %resid.1, bf16[1,4096]{1,0:T(2,128)(2,1)} %reshape.12.gain, bf16[256,768]{1,0:T(8,128)(2,1)} %grad_q.1, bf16[768,4096]{1,0:T(8,128)(2,1)} %w_query.1, bf16[256,4096]{1,0:T(8,128)(2,1)} %grad_in.1), custom_call_target="tpu_custom_call" | custom-call | tf_op jit(solution)/shard_map/pallas_call | solution.py:309
  78.9 0.0 copy-start.1
  78.9 0.0 copy-start
  78.9 2.8 %copy.11 = f32[96,4096]{1,0:T(8,128)} copy(f32[96,4096]{1,0:T(8,128)} %get-tuple-element.12) | data formatting | bytes 3145728
  81.7 0.0 copy-done.1
  81.7 0.6 copy.12
  82.3 0.0 copy-done
  82.3 1.3 %copy.13 = bf16[256,4096]{1,0:T(8,128)(2,1)} copy(bf16[256,4096]{1,0:T(8,128)(2,1)S(1)} %copy-done) | data formatting | bytes 4194304
Async XLA Ops:
  78.9 2.8 %copy-start.1 = (f32[1,4096]{1,0:T(1,128)S(1)}, f32[1,4096]{1,0:T(1,128)}, u32[]{:S(2)}) copy-start(f32[1,4096]{1,0:T(1,128)} %get-tuple-element.7) | copy-start | bytes 49156
  78.9 3.4 %copy-start = (bf16[256,4096]{1,0:T(8,128)(2,1)S(1)}, bf16[256,4096]{1,0:T(8,128)(2,1)}, u32[]{:S(2)}) copy-start(bf16[256,4096]{1,0:T(8,128)(2,1)} %get-tuple-element.14) | copy-start | bytes 6291460

commit v2 on v1

--- a/solution.py
+++ b/solution.py
@@ -190,35 +190,43 @@
             copy_o(from_mate, c).wait_recv()
             out_copy(from_mate, c).start()
 
-    @pl.loop(0, steps)
+    def pass_on(k):
+        b = rows_of(2 * k + 1 - h)
+        copy_o(part, 2 * k + 1 - h).wait_recv()
+        part[b, :] = (part[b, :].astype(F32) + from_mate[b, :].astype(F32)).astype(BF16)
+        copy_p(part, 2 * k + 1 - h).start()
+
+    def finish(k):
+        a = 2 * k + h
+        copy_o(part, a).wait_recv()
+        copy_p(part, a).wait_recv()
+        r = rows_of(a)
+        inv_rms, unit, _ = norm_rows(rv[r, :], gain_f)
+        dnormed = part[r, :].astype(F32) + from_mate[r, :].astype(F32)
+        dnormed = dnormed + from_peer[r, :].astype(F32)
+        gacc[...] += jnp.sum(dnormed * unit, axis=0, keepdims=True)
+        dunit = dnormed * gain_f
+        mean = jnp.mean(dunit * unit, axis=-1, keepdims=True)
+        part[r, :] = (
+            giv[r, :].astype(F32) + inv_rms * (dunit - unit * mean)
+        ).astype(BF16)
+        copy_p(part, a).start()
+        copy_o(part, a).start()
+        out_copy(part, a).start()
+
+    @pl.loop(0, steps + 1)
     def _(k):
-        @pl.when(is_inner)
-        def _():
-            a, b = 2 * k + h, 2 * k + 1 - h
-            copy_o(part, b).wait_recv()
-            part[rows_of(b), :] = (
-                part[rows_of(b), :].astype(F32) + from_mate[rows_of(b), :].astype(F32)
-            ).astype(BF16)
-            copy_p(part, b).start()
-            copy_o(part, a).wait_recv()
-            copy_p(part, a).wait_recv()
-            r = rows_of(a)
-            inv_rms, unit, _ = norm_rows(rv[r, :], gain_f)
-            dnormed = part[r, :].astype(F32) + from_mate[r, :].astype(F32)
-            dnormed = dnormed + from_peer[r, :].astype(F32)
-            gacc[...] += jnp.sum(dnormed * unit, axis=0, keepdims=True)
-            dunit = dnormed * gain_f
-            mean = jnp.mean(dunit * unit, axis=-1, keepdims=True)
-            part[r, :] = (
-                giv[r, :].astype(F32) + inv_rms * (dunit - unit * mean)
-            ).astype(BF16)
-            copy_p(part, a).start()
-            copy_o(part, a).start()
-            out_copy(part, a).start()
-
-            @pl.when(k > 0)
-            def _():
-                forward(k - 1)
+        @pl.when(jnp.logical_and(is_inner, k < steps))
+        def _():
+            pass_on(k)
+
+        @pl.when(jnp.logical_and(is_inner, k > 0))
+        def _():
+            finish(k - 1)
+
+        @pl.when(jnp.logical_and(is_inner, k > 1))
+        def _():
+            forward(k - 2)
 
         @pl.when(jnp.logical_and(is_outer, k > 2))
         def _():
@@ -280,7 +288,7 @@
 
     @pl.when(is_outer)
     def _():
-        for k in range(steps - 3, steps):
+        for k in range(steps - 2, steps):
             collect(k)
         z_wait(0)
         z_wait(1)

time: 83.9 us -> 77.2 us (0.920)
  Pallas kernels: 76.9 us -> 70.2 us
    pallas_call x1, Pallas kernels: 76.9 us -> 70.2 us  [fused(): pl.pallas_call(functools.partial(kernel, n_dp, n_tp), out_shape=(jax.Shap...]
where the time goes in v2:
time: 77.2 us; the launch traced here: 76.9 us
  Pallas kernels  70.2 us (91%)
  local copies, waits for them, and re-layouts  6.05 us (8%)
    pallas_call x1, Pallas kernels, fused(): pl.pallas_call(functools.partial(kernel, n_dp, n_tp), out_shape=(jax.Shap...  70.2 us
    unnamed x7, local copies, waits for them, and re-layouts  4.74 us

profile of v2, /device:TPU:0, one launch (start us, length us, event | category | flops | bytes accessed | tf_op | source)
XLA Modules:
  0.0 76.9 jit_solution(15025582604231926536)
XLA Ops:
  0.6 1.3 %reshape.12.gain = bf16[1,4096]{1,0:T(2,128)(2,1)} reshape(bf16[4096]{0:T(1024)(128)(2,1)} %param.6) | data formatting | bytes 16384 | tf_op jit(solution)/shard_map/reshape | solution.py:355
  1.9 70.2 %shard_map.76 = (f32[96,4096]{1,0:T(8,128)}, f32[1,4096]{1,0:T(1,128)}, bf16[256,4096]{1,0:T(8,128)(2,1)}) custom-call(bf16[256,4096]{1,0:T(8,128)(2,1)} %resid.1, bf16[1,4096]{1,0:T(2,128)(2,1)} %reshape.12.gain, bf16[256,768]{1,0:T(8,128)(2,1)} %grad_q.1, bf16[768,4096]{1,0:T(8,128)(2,1)} %w_query.1, bf16[256,4096]{1,0:T(8,128)(2,1)} %grad_in.1), custom_call_target="tpu_custom_call" | custom-call | tf_op jit(solution)/shard_map/pallas_call | solution.py:317
  72.1 0.0 copy-start.1
  72.1 0.0 copy-start
  72.1 2.8 %copy.11 = f32[96,4096]{1,0:T(8,128)} copy(f32[96,4096]{1,0:T(8,128)} %get-tuple-element.12) | data formatting | bytes 3145728
  74.9 0.0 copy-done.1
  74.9 0.6 copy.12
  75.6 0.0 copy-done
  75.6 1.3 %copy.13 = bf16[256,4096]{1,0:T(8,128)(2,1)} copy(bf16[256,4096]{1,0:T(8,128)(2,1)S(1)} %copy-done) | data formatting | bytes 4194304
Async XLA Ops:
  72.1 2.8 %copy-start.1 = (f32[1,4096]{1,0:T(1,128)S(1)}, f32[1,4096]{1,0:T(1,128)}, u32[]{:S(2)}) copy-start(f32[1,4096]{1,0:T(1,128)} %get-tuple-element.7) | copy-start | bytes 49156
  72.1 3.4 %copy-start = (bf16[256,4096]{1,0:T(8,128)(2,1)S(1)}, bf16[256,4096]{1,0:T(8,128)(2,1)}, u32[]{:S(2)}) copy-start(bf16[256,4096]{1,0:T(8,128)(2,1)} %get-tuple-element.14) | copy-start | bytes 6291460
